TPU v7x, 32 devices: a whole 2x2x4 slice. The times are simulated.
32 devices in a mesh: ctx: 16 (over z, y, x), head: 2 (over core).
Axes of the slice: x: 2, y: 2, z: 4, core: 2. Of those that a mesh axis runs over, the one named last changes fastest.
Arguments:
- query: bfloat16 [2048, 384], P('ctx', 'head'), may hold values from -48 to 48
- key_nope: bfloat16 [2048, 256], P('ctx', 'head'), may hold values from -8 to 8
- key_rope: bfloat16 [2048, 64], P('ctx'), may hold values from -8 to 8
- value: bfloat16 [2048, 256], P('ctx', 'head'), may hold values from -6 to 6
- d_out: bfloat16 [2048, 256], P('ctx', 'head'), may hold values from -288 to 288
- positions: int32 [2048], P('ctx'), may hold values from 0 to 2047, as said below
- segments: int32 [2048], replicated, may hold values from 0 to 3, never falling along the last dimension, each value on 1 to 1024 neighbouring positions
Outputs:
- d_query: bfloat16 [2048, 384], P('ctx', 'head')
- d_key_nope: bfloat16 [2048, 256], P('ctx', 'head')
- d_key_rope: bfloat16 [2048, 64], P('ctx')
- d_value: bfloat16 [2048, 256], P('ctx', 'head')
Inputs may be any that keep to these rules, and one draw needn't show every extreme that they name: A permutation of 0 to 2047 made of aligned blocks of 32 rows holding 32 consecutive positions in order.
All inputs are finite; a program needn't handle non-finite values.
Results may differ from a plain program's by a relative error of at most 0.0049.
Values may be sent and summed in bfloat16 or wider, within the bound.
A program may use at most 64 MiB of HBM per device.

v0:
```python
import math

import jax
import jax.numpy as jnp
from jax import lax
from jax.sharding import PartitionSpec as P

NOPE = 128
ROPE = 64
VD = 128
QK = 192


clip_ratio = 0.25
block_limit = 1024


def split_heads(array, width):
    return array.reshape(array.shape[0], -1, width)


def make_keys(nope_rows, rope_rows):
    nope_three = split_heads(nope_rows, NOPE)
    rope_three = rope_rows[:, None, :]
    return jnp.concatenate([nope_three, rope_three], axis=2)


def visible(query_place, query_doc, key_place, key_doc):
    return (query_doc[:, None] == key_doc[None, :]) & (key_place[None, :] <= query_place[:, None])


def over_blocks(advance, carried, pieces, offset=0):
    row_count = pieces[0].shape[0]
    blocks = row_count // block_limit
    parts = jax.tree.map(
        lambda array: array.reshape((blocks, block_limit) + array.shape[1:]), pieces
    )

    def visitor(state_now, part_now):
        return (advance(state_now, part_now, offset), None)

    carried, unused = lax.scan(visitor, carried, parts)
    return carried


def shards(query, key_nope, key_rope, value, d_out, positions, segments):
    softmax_scale = 1.0 / math.sqrt(QK)
    documents = jnp.take(segments, positions)
    local_rows = query.shape[0]
    heads_here = query.shape[1] // QK
    query_three = split_heads(query, QK)
    dout_three = split_heads(d_out, VD)

    def soft_advance(carried, pieces, offset):
        row_max, row_sum, weighted = carried
        piece_nope, piece_rope, piece_value, piece_place, piece_doc = pieces
        key_rows = make_keys(piece_nope, piece_rope)
        scores = (
            jnp.einsum("qhd,khd->hqk", query_three, key_rows, preferred_element_type=jnp.float32)
            * softmax_scale
        )
        allowed = visible(positions, documents, piece_place, piece_doc)[None]
        scores = jnp.where(allowed, scores, -jnp.inf)
        new_max = jnp.maximum(row_max, jnp.max(scores, axis=2))
        safe_max = jnp.where(new_max == -jnp.inf, 0.0, new_max)
        exponent = jnp.exp(scores - safe_max[:, :, None])
        d_prob = jnp.einsum(
            "qhv,khv->hqk",
            dout_three,
            split_heads(piece_value, VD),
            preferred_element_type=jnp.float32,
        )
        shrink = jnp.exp(row_max - safe_max)
        return (
            new_max,
            row_sum * shrink + jnp.sum(exponent, axis=2),
            weighted * shrink + jnp.sum(exponent * d_prob, axis=2),
        )

    soft_init = (
        jnp.full((heads_here, local_rows), -jnp.inf, jnp.float32),
        jnp.zeros((heads_here, local_rows), jnp.float32),
        jnp.zeros((heads_here, local_rows), jnp.float32),
    )
    soft_state = over_blocks(
        soft_advance,
        soft_init,
        (
            lax.all_gather(key_nope, "ctx", axis=0, tiled=True),
            lax.all_gather(key_rope, "ctx", axis=0, tiled=True),
            lax.all_gather(value, "ctx", axis=0, tiled=True),
            lax.all_gather(positions, "ctx", axis=0, tiled=True),
            lax.all_gather(documents, "ctx", axis=0, tiled=True),
        ),
        jnp.int32(0),
    )
    row_max, row_sum, weighted = soft_state
    log_total = row_max + jnp.log(row_sum)
    row_delta = weighted / row_sum

    def query_advance(grad_query, pieces, offset):
        piece_nope, piece_rope, piece_value, piece_place, piece_doc = pieces
        key_rows = make_keys(piece_nope, piece_rope)
        scores = (
            jnp.einsum("qhd,khd->hqk", query_three, key_rows, preferred_element_type=jnp.float32)
            * softmax_scale
        )
        allowed = visible(positions, documents, piece_place, piece_doc)[None]
        weights = jnp.exp(jnp.where(allowed, scores, -jnp.inf) - log_total[:, :, None])
        d_prob = jnp.einsum(
            "qhv,khv->hqk",
            dout_three,
            split_heads(piece_value, VD),
            preferred_element_type=jnp.float32,
        )
        d_score = (weights * (d_prob - row_delta[:, :, None])).astype(jnp.bfloat16)
        return (
            grad_query
            + jnp.einsum("hqk,khd->qhd", d_score, key_rows, preferred_element_type=jnp.float32)
            * softmax_scale
        )

    query_init = jnp.zeros((local_rows, heads_here, QK), jnp.float32)
    grad_query = over_blocks(
        query_advance,
        query_init,
        (
            lax.all_gather(key_nope, "ctx", axis=0, tiled=True),
            lax.all_gather(key_rope, "ctx", axis=0, tiled=True),
            lax.all_gather(value, "ctx", axis=0, tiled=True),
            lax.all_gather(positions, "ctx", axis=0, tiled=True),
            lax.all_gather(documents, "ctx", axis=0, tiled=True),
        ),
        jnp.int32(0),
    )
    local_keys = make_keys(key_nope, key_rope)
    value_three = split_heads(value, VD)

    def key_advance(carried, pieces, offset):
        grad_key, grad_value = carried
        piece_query, piece_dout, piece_log, piece_delta, piece_place, piece_doc = pieces
        piece_query_three = split_heads(piece_query, QK)
        piece_dout_three = split_heads(piece_dout, VD)
        scores = (
            jnp.einsum(
                "qhd,khd->hqk", piece_query_three, local_keys, preferred_element_type=jnp.float32
            )
            * softmax_scale
        )
        allowed = visible(piece_place, piece_doc, positions, documents)[None]
        weights = jnp.exp(jnp.where(allowed, scores, -jnp.inf) - piece_log.T[:, :, None])
        d_prob = jnp.einsum(
            "qhv,khv->hqk", piece_dout_three, value_three, preferred_element_type=jnp.float32
        )
        d_score = (weights * (d_prob - piece_delta.T[:, :, None])).astype(jnp.bfloat16)
        grad_key = (
            grad_key
            + jnp.einsum(
                "hqk,qhd->khd", d_score, piece_query_three, preferred_element_type=jnp.float32
            )
            * softmax_scale
        )
        grad_value = grad_value + jnp.einsum(
            "hqk,qhv->khv",
            weights.astype(jnp.bfloat16),
            piece_dout_three,
            preferred_element_type=jnp.float32,
        )
        return (grad_key, grad_value)

    key_init = (
        jnp.zeros((local_rows, heads_here, QK), jnp.float32),
        jnp.zeros((local_rows, heads_here, VD), jnp.float32),
    )
    grad_key, grad_value = over_blocks(
        key_advance,
        key_init,
        (
            lax.all_gather(query.astype(jnp.float32), "ctx", axis=0, tiled=True).astype(
                jnp.bfloat16
            ),
            lax.all_gather(d_out.astype(jnp.float32), "ctx", axis=0, tiled=True).astype(
                jnp.bfloat16
            ),
            lax.all_gather(log_total.T, "ctx", axis=0, tiled=True),
            lax.all_gather(row_delta.T, "ctx", axis=0, tiled=True),
            lax.all_gather(positions, "ctx", axis=0, tiled=True),
            lax.all_gather(documents, "ctx", axis=0, tiled=True),
        ),
        jnp.int32(0),
    )
    grad_nope = grad_key[:, :, :NOPE]
    rope_part = jnp.sum(grad_key[:, :, NOPE:], axis=1)
    local_squares = (
        jnp.sum(jnp.square(grad_query))
        + jnp.sum(jnp.square(grad_nope))
        + jnp.sum(jnp.square(grad_value))
    )
    rope_summed = lax.psum(rope_part, "head")
    first_head = (lax.axis_index("head") == 0).astype(jnp.float32)
    local_squares = local_squares + first_head * jnp.sum(jnp.square(rope_summed))
    total = lax.psum(local_squares, ("ctx", "head"))
    count_all = float(
        local_rows
        * lax.axis_size("ctx")
        * (heads_here * lax.axis_size("head") * (QK + NOPE + VD) + ROPE)
    )
    factor = jnp.minimum(1.0, clip_ratio * math.sqrt(count_all) / jnp.sqrt(total))
    d_key_rope = (rope_summed * factor).astype(jnp.bfloat16)
    d_query = (grad_query * factor).astype(jnp.bfloat16).reshape(local_rows, heads_here * QK)
    d_key_nope = (grad_nope * factor).astype(jnp.bfloat16).reshape(local_rows, heads_here * NOPE)
    d_value = (grad_value * factor).astype(jnp.bfloat16).reshape(local_rows, heads_here * VD)
    return (d_query, d_key_nope, d_key_rope, d_value)


def solution(mesh):
    return jax.shard_map(
        shards,
        mesh=mesh,
        in_specs=(
            P("ctx", "head"),
            P("ctx", "head"),
            P("ctx", None),
            P("ctx", "head"),
            P("ctx", "head"),
            P("ctx"),
            P(),
        ),
        out_specs=(P("ctx", "head"), P("ctx", "head"), P("ctx", None), P("ctx", "head")),
        check_vma=False,
    )
```

profile of v0, /device:TPU:0, one launch (start us, length us, event | category | flops | bytes accessed | tf_op | source)
XLA Modules:
  0.0 411.0 jit_solution(17462087313874825854)
XLA Ops:
  0.7 45.8 %all_gather.34 = bf16[2048,128]{1,0:T(8,128)(2,1)S(1)} all-gather(bf16[128,128]{1,0:T(8,128)(2,1)} %param.14), channel_id=1, replica_groups=mesh['ctx'=16,'head'=2] {'ctx'}, dimensions={0}, use_global_device_ids=true | all-gather | bytes 557056 | tf_op jit(solution)/shard_map/all_gather | solution.py:128
  46.4 37.0 %all_gather.35 = bf16[2048,64]{0,1:T(8,128)(2,1)S(1)} all-gather(bf16[128,64]{0,1:T(8,128)(2,1)S(1)} %copy-done.4), channel_id=1, replica_groups=mesh['ctx'=16,'head'=2] {'ctx'}, dimensions={0}, use_global_device_ids=true | all-gather | bytes 278528 | tf_op jit(solution)/shard_map/all_gather | solution.py:129
  83.7 0.6 copy-done.6
  84.3 1.1 gather_fusion
  85.5 37.4 %all-gather.2 = s32[16,1,128]{2,1,0:T(1,128)S(1)} all-gather(s32[1,1,128]{2,1,0:T(1,128)S(1)} %bitcast.246), channel_id=1, replica_groups=mesh['ctx'=16,'head'=2] {'ctx'}, dimensions={0}, use_global_device_ids=true | all-gather | bytes 8704 | tf_op jit(solution)/shard_map/all_gather | solution.py:132
  122.9 0.5 broadcast.162
  123.4 0.7 reduce.12
  124.1 35.6 %all-gather.3 = s32[16,1,128]{2,1,0:T(1,128)S(1)} all-gather(s32[1,1,128]{2,1,0:T(1,128)S(1)} %bitcast.245), channel_id=1, replica_groups=mesh['ctx'=16,'head'=2] {'ctx'}, dimensions={0}, use_global_device_ids=true | all-gather | bytes 8704 | tf_op jit(solution)/shard_map/all_gather | solution.py:131
  159.7 0.7 reduce.13
  160.5 40.5 %all_gather.38 = bf16[2048,128]{1,0:T(8,128)(2,1)S(1)} all-gather(bf16[128,128]{1,0:T(8,128)(2,1)S(1)} %copy-done.2), channel_id=1, replica_groups=mesh['ctx'=16,'head'=2] {'ctx'}, dimensions={0}, use_global_device_ids=true | all-gather | bytes 557056 | tf_op jit(solution)/shard_map/all_gather | solution.py:130
  201.0 2.0 while.39
  203.0 2.0 while.40
  203.3 0.7 fusion.120
  204.3 0.7 fusion.120
  205.0 0.6 multiply_reduce_fusion
  205.7 40.5 %all_gather.39 = bf16[2048,192]{0,1:T(8,128)(2,1)S(1)} all-gather(bf16[128,192]{0,1:T(8,128)(2,1)S(1)} %bitcast.242), channel_id=1, replica_groups=mesh['ctx'=16,'head'=2] {'ctx'}, dimensions={0}, use_global_device_ids=true | all-gather | bytes 835584 | tf_op jit(solution)/shard_map/all_gather | solution.py:179
  246.2 0.5 copy.24
  246.8 0.6 copy-done.3
  247.6 37.5 %all-gather = f32[1,2048]{1,0:T(1,128)S(1)} all-gather(f32[1,128]{1,0:T(1,128)S(1)} %get-tuple-element.874), channel_id=2, replica_groups=mesh['ctx'=16,'head'=2] {'ctx'}, dimensions={1}, use_global_device_ids=true | all-gather | bytes 8704 | tf_op jit(solution)/shard_map/all_gather | solution.py:185
  285.0 38.3 %all_gather.41 = bf16[2048,128]{1,0:T(8,128)(2,1)S(1)} all-gather(bf16[128,128]{1,0:T(8,128)(2,1)S(1)} %bitcast.227), channel_id=1, replica_groups=mesh['ctx'=16,'head'=2] {'ctx'}, dimensions={0}, use_global_device_ids=true | all-gather | bytes 557056 | tf_op jit(solution)/shard_map/all_gather | solution.py:182
  323.3 37.5 %all-gather.1 = f32[1,2048]{1,0:T(1,128)S(1)} all-gather(f32[1,128]{1,0:T(1,128)S(1)} %get-tuple-element.873), channel_id=3, replica_groups=mesh['ctx'=16,'head'=2] {'ctx'}, dimensions={1}, use_global_device_ids=true | all-gather | bytes 8704 | tf_op jit(solution)/shard_map/all_gather | solution.py:186
  360.8 2.7 while.41
  361.3 0.5 fusion.129
  362.7 0.5 fusion.129
  363.6 0.6 multiply_reduce_fusion.2
  365.5 0.6 multiply_reduce_fusion.1
  366.8 3.4 psum.14
  370.2 0.6 multiply_reduce_fusion.3
  371.5 36.8 %psum.15 = f32[]{:T(128)} all-reduce(f32[]{:T(128)S(6)} %add.53), channel_id=1, replica_groups=mesh['ctx'=16,'head'=2] {'ctx','head'}, use_global_device_ids=true, to_apply=%region_14.15 | all-reduce | flops 1 | bytes 8 | tf_op jit(solution)/shard_map/psum | solution.py:202
  409.0 0.6 fusion.82
  409.7 0.6 fusion.83
  410.4 0.6 multiply_convert_fusion.3
  (65 shorter events, 4.8 us)
Async XLA Ops:
  0.6 83.7 %copy-start = (s32[2048]{0:T(1024)S(1)}, s32[2048]{0:T(1024)}, u32[]{:S(2)}) copy-start(s32[2048]{0:T(1024)} %param.19) | copy-start | bytes 24580
  0.7 45.8 %copy-start.4 = (bf16[128,64]{0,1:T(8,128)(2,1)S(1)}, bf16[128,64]{0,1:T(8,128)(2,1)}, u32[]{:S(2)}) copy-start(bf16[128,64]{0,1:T(8,128)(2,1)} %param.15) | copy-start | bytes 49156
  83.7 0.7 copy-start.6
  124.1 36.4 %copy-start.2 = (bf16[128,128]{1,0:T(8,128)(2,1)S(1)}, bf16[128,128]{1,0:T(8,128)(2,1)}, u32[]{:S(2)}) copy-start(bf16[128,128]{1,0:T(8,128)(2,1)} %param.16) | copy-start | bytes 98308
  160.4 40.6 %copy-start.1 = (bf16[128,128]{1,0:T(8,128)(2,1)S(1)}, bf16[128,128]{1,0:T(8,128)(2,1)}, u32[]{:S(2)}) copy-start(bf16[128,128]{1,0:T(8,128)(2,1)} %param.17) | copy-start | bytes 98308
  160.5 40.5 %copy-start.5 = (bf16[128,192]{0,1:T(8,128)(2,1)S(1)}, bf16[128,192]{0,1:T(8,128)(2,1)}, u32[]{:S(2)}) copy-start(bf16[128,192]{0,1:T(8,128)(2,1)} %param.13) | copy-start | bytes 147460
  246.7 0.8 copy-start.3
where the time goes:
time: 412 us; the launch traced here: 411 us
  blocking collectives  390 us (95%)
  other arithmetic  6.09 us (1%)
  matrix products  5.77 us (1%)
  local copies, waits for them, and re-layouts  4.48 us (1%)
  between operations  4.17 us (1%)
    all_gather x1, blocking collectives, shards(): lax.all_gather(key_nope, 'ctx', axis=0, tiled=True)  45.8 us
    all_gather x1, blocking collectives, shards(): lax.all_gather(value, 'ctx', axis=0, tiled=True)  40.5 us
    all_gather x1, blocking collectives, shards(): lax.all_gather(query.astype(jnp.float32), 'ctx', axis=0, tiled=True)  40.5 us
    all_gather x1, blocking collectives, shards(): lax.all_gather(d_out.astype(jnp.float32), 'ctx', axis=0, tiled=True)  38.3 us
    all_gather x1, blocking collectives, shards(): lax.all_gather(log_total.T, 'ctx', axis=0, tiled=True)  37.5 us
    all_gather x1, blocking collectives, shards(): lax.all_gather(row_delta.T, 'ctx', axis=0, tiled=True)  37.5 us
    all_gather x1, blocking collectives, shards(): lax.all_gather(documents, 'ctx', axis=0, tiled=True)  37.4 us
    all_gather x1, blocking collectives, shards(): lax.all_gather(key_rope, 'ctx', axis=0, tiled=True)  37 us

commit v1 on v0

v1 whole, which is shorter than its diff:
```python
import functools
import math

import jax
import jax.numpy as jnp
from jax import lax
from jax.experimental import pallas as pl
from jax.experimental.pallas import tpu as pltpu
from jax.sharding import PartitionSpec as P

NOPE = 128
ROPE = 64
VD = 128
QK = 192
DOCS = 4
CLIP = 0.25
MESH = pl.DeviceIdType.MESH
HIDDEN = -3.0e38
LOWEST = -1.0e30


def grid_of(count):
    width = 1 << (int(math.log2(count)) // 2)
    return count // width, width


def kernel(
    A, B, H, count_all,
    q_in, kn_in, kr_in, v_in, do_in, pos_in, seg_in,
    dq_out, dkn_out, dkr_out, dv_out,
    qb, dob, pqb, knb, krb, vb, pkb,
    stat, statb,
    dqs, dqr, dks, dkr, dvs, dvr, drs, drr,
    n1, n2,
    own_sem, qsend, qrecv, ksend, krecv, ssend, srecv,
    dqsend, dqrecv, dksend, dkrecv, drsend, drrecv, n1send, n1recv, n2send, n2recv,
):
    R = q_in.shape[0]
    NQ, NK = A * R, B * R
    scale = 1.0 / math.sqrt(QK)
    ctx = lax.axis_index("ctx")
    head = lax.axis_index("head")
    a, b = ctx // B, ctx % B

    def a_peer(j):
        return {"ctx": lax.rem(a + j, A) * B + b, "head": head}

    def b_peer(j, g=0):
        return {"ctx": a * B + lax.rem(b + j, B), "head": lax.rem(head + g, H)}

    def remote(src, dst, send, recv, peer):
        return pltpu.make_async_remote_copy(
            src_ref=src, dst_ref=dst, send_sem=send, recv_sem=recv,
            device_id=peer, device_id_type=MESH,
        )

    own = []
    for i, (src, dst) in enumerate((
        (q_in, qb.at[0]), (do_in, dob.at[0]), (pos_in, pqb.at[0]),
        (kn_in, knb.at[0]), (kr_in, krb.at[0]), (v_in, vb.at[0]), (pos_in, pkb.at[0]),
    )):
        copy = pltpu.make_async_copy(src, dst, own_sem.at[i])
        copy.start()
        own.append(copy)

    barrier = pltpu.get_barrier_semaphore()
    peers = [a_peer(j) for j in range(1, A)]
    peers += [b_peer(j, g) for g in range(H) for j in range(B) if (j, g) != (0, 0)]
    for peer in peers:
        pl.semaphore_signal(barrier, inc=1, device_id=peer, device_id_type=MESH)
    pl.semaphore_wait(barrier, len(peers))

    sends = []
    q_copies, k_copies = [], []
    for j in range(1, max(A, B)):
        if j < B:
            for i, (src, buf) in enumerate(((kn_in, knb), (kr_in, krb), (pos_in, pkb), (v_in, vb))):
                k_copies.append(remote(src, buf.at[j], ksend.at[i, j], krecv.at[i, j], b_peer(j)))
                k_copies[-1].start()
        if j < A:
            for i, (src, buf) in enumerate(((q_in, qb), (pos_in, pqb), (do_in, dob))):
                q_copies.append(remote(src, buf.at[j], qsend.at[i, j], qrecv.at[i, j], a_peer(j)))
                q_copies[-1].start()
    sends += q_copies + k_copies

    for copy in own:
        copy.wait()
    for copy in q_copies + k_copies:
        copy.wait_recv()

    q = qb[...].reshape(NQ, QK)
    do = dob[...].reshape(NQ, VD)
    k = jnp.concatenate([knb[...].reshape(NK, NOPE), krb[...].reshape(NK, ROPE)], axis=1)
    v = vb[...].reshape(NK, VD)
    pos_q = jnp.concatenate([pqb[j] for j in range(A)], axis=1)
    seg = seg_in[...]
    start_q = jnp.zeros_like(pos_q)
    for doc in range(1, DOCS):
        first = jnp.sum((seg < doc).astype(jnp.int32))
        start_q = jnp.where(pos_q >= first, first, start_q)
    cols = []
    for j in range(B):
        cols.append(jnp.transpose(jnp.broadcast_to(pkb[j], (R, R))))
    pos_k = jnp.concatenate(cols, axis=0)
    pos_k = jnp.concatenate([pos_k] * A, axis=1)

    nt = (((1,), (1,)), ((), ()))
    s = lax.dot_general(k, q, nt, preferred_element_type=jnp.float32) * scale
    dp = lax.dot_general(v, do, nt, preferred_element_type=jnp.float32)
    vis = (pos_k <= pos_q) & (pos_k >= start_q)
    s = jnp.where(vis, s, HIDDEN)
    m = jnp.maximum(jnp.max(s, axis=0, keepdims=True), LOWEST)
    e = jnp.exp(s - m)
    l = jnp.sum(e, axis=0, keepdims=True)
    wd = jnp.sum(e * dp, axis=0, keepdims=True)

    stat[...] = jnp.concatenate([m, l, wd], axis=1)
    s_copies = []
    for j in range(1, A):
        s_copies.append(remote(stat, statb.at[j], ssend.at[j], srecv.at[j], a_peer(j)))
        s_copies[-1].start()
    sends += s_copies
    ms, ls, wds = [m], [l], [wd]
    for copy in s_copies:
        copy.wait_recv()
    for j in range(1, A):
        got = statb[j]
        parts = []
        for i in range(3):
            one = got[:, i * NQ:(i + 1) * NQ]
            cut = ((A - j) % A) * R
            parts.append(jnp.concatenate([one[:, cut:], one[:, :cut]], axis=1))
        ms.append(parts[0])
        ls.append(parts[1])
        wds.append(parts[2])
    top = functools.reduce(jnp.maximum, ms)
    shrink = [jnp.exp(x - top) for x in ms]
    total_l = sum(x * y for x, y in zip(ls, shrink))
    total_wd = sum(x * y for x, y in zip(wds, shrink))
    inverse = 1.0 / total_l
    f = shrink[0] * inverse
    delta = total_wd * inverse

    w = e * f
    ds = (w * (dp - delta)).astype(jnp.bfloat16)
    wb = w.astype(jnp.bfloat16)
    dk = jnp.dot(ds, q, preferred_element_type=jnp.float32) * scale
    dv = jnp.dot(wb, do, preferred_element_type=jnp.float32)
    dks[...] = dk[:, :NOPE].astype(jnp.bfloat16).reshape(B, R, NOPE)
    drs[...] = dk[:, NOPE:].astype(jnp.bfloat16).reshape(B, R, ROPE)
    dvs[...] = dv.astype(jnp.bfloat16).reshape(B, R, VD)
    g_copies = []
    for j in range(1, B):
        peer = b_peer(B - j)
        g_copies.append(remote(dks.at[j], dkr.at[j], dksend.at[0, j], dkrecv.at[0, j], peer))
        g_copies.append(remote(dvs.at[j], dvr.at[j], dksend.at[1, j], dkrecv.at[1, j], peer))
    rope_slot = b * H + head
    for j in range(B):
        for g in range(H):
            if (j, g) == (0, 0):
                continue
            peer = b_peer(B - j, H - g)
            g_copies.append(
                remote(drs.at[j], drr.at[rope_slot], drsend.at[j, g], drrecv.at[j, g], peer)
            )
    for copy in g_copies:
        copy.start()
    dq = lax.dot_general(ds, k, (((0,), (0,)), ((), ())), preferred_element_type=jnp.float32) * scale
    dqs[...] = dq.astype(jnp.bfloat16).reshape(A, R, QK)
    q_grads = []
    for j in range(1, A):
        q_grads.append(remote(dqs.at[j], dqr.at[j], dqsend.at[j], dqrecv.at[j], a_peer(A - j)))
        q_grads[-1].start()
    drr[rope_slot] = dk[:R, NOPE:].astype(jnp.bfloat16)

    for copy in g_copies[: 2 * (B - 1)]:
        copy.wait_recv()
    gk = dk[:R, :NOPE]
    gv = dv[:R]
    for j in range(1, B):
        gk = gk + dkr[j].astype(jnp.float32)
        gv = gv + dvr[j].astype(jnp.float32)
    for j in range(B):
        for g in range(H):
            if (j, g) == (0, 0):
                continue
            slot = lax.rem(b + j, B) * H + lax.rem(head + g, H)
            remote(drs.at[j], drr.at[slot], drsend.at[j, g], drrecv.at[j, g], b_peer(j, g)).wait_recv()
    gr = drr[0].astype(jnp.float32)
    for i in range(1, B * H):
        gr = gr + drr[i].astype(jnp.float32)
    for copy in q_grads:
        copy.wait_recv()
    gq = dq[:R]
    for j in range(1, A):
        gq = gq + dqr[j].astype(jnp.float32)

    def squares(x):
        return jnp.sum(x * x, axis=0, keepdims=True)

    qs, rs = squares(gq), squares(gr)
    first_head = (head == 0).astype(jnp.float32)
    narrow = qs[:, NOPE:] + rs * first_head
    mine = squares(gk) + squares(gv) + qs[:, :NOPE] + jnp.concatenate(
        [narrow, jnp.zeros_like(narrow)], axis=1)
    n1[rope_slot] = mine
    c1 = []
    for j in range(B):
        for g in range(H):
            if (j, g) == (0, 0):
                continue
            c1.append(remote(n1.at[rope_slot], n1.at[rope_slot], n1send.at[j, g], n1recv.at[j, g],
                             b_peer(B - j, H - g)))
            c1[-1].start()
    for j in range(B):
        for g in range(H):
            if (j, g) == (0, 0):
                continue
            slot = lax.rem(b + j, B) * H + lax.rem(head + g, H)
            remote(n1.at[slot], n1.at[slot], n1send.at[j, g], n1recv.at[j, g], b_peer(j, g)).wait_recv()
    part = n1[0]
    for i in range(1, B * H):
        part = part + n1[i]
    n2[a] = part
    c2 = []
    for j in range(1, A):
        c2.append(remote(n2.at[a], n2.at[a], n2send.at[j], n2recv.at[j], a_peer(A - j)))
        c2[-1].start()
    for j in range(1, A):
        slot = lax.rem(a + j, A)
        remote(n2.at[slot], n2.at[slot], n2send.at[j], n2recv.at[j], a_peer(j)).wait_recv()
    part = n2[0]
    for i in range(1, A):
        part = part + n2[i]
    total = jnp.sum(part, axis=1, keepdims=True)
    factor = jnp.minimum(1.0, CLIP * math.sqrt(count_all) / jnp.sqrt(total))
    dq_out[...] = (gq * factor).astype(jnp.bfloat16)
    dkn_out[...] = (gk * factor).astype(jnp.bfloat16)
    dkr_out[...] = (gr * factor).astype(jnp.bfloat16)
    dv_out[...] = (gv * factor).astype(jnp.bfloat16)
    for copy in sends + g_copies + q_grads + c1 + c2:
        copy.wait_send()


def shards(query, key_nope, key_rope, value, d_out, positions, segments):
    R = query.shape[0]
    n, H = lax.axis_size("ctx"), lax.axis_size("head")
    A, B = grid_of(n)
    NQ = A * R
    count_all = float(R * n * (H * (QK + NOPE + VD) + ROPE))
    bf, f32 = jnp.bfloat16, jnp.float32
    any_spec = pl.BlockSpec(memory_space=pl.ANY)
    vmem = pl.BlockSpec(memory_space=pltpu.VMEM)
    dma = pltpu.SemaphoreType.DMA
    return pl.pallas_call(
        functools.partial(kernel, A, B, H, count_all),
        out_shape=(
            jax.ShapeDtypeStruct((R, QK), bf),
            jax.ShapeDtypeStruct((R, NOPE), bf),
            jax.ShapeDtypeStruct((R, ROPE), bf),
            jax.ShapeDtypeStruct((R, VD), bf),
        ),
        in_specs=[any_spec] * 6 + [vmem],
        out_specs=(vmem,) * 4,
        scratch_shapes=[
            pltpu.VMEM((A, R, QK), bf), pltpu.VMEM((A, R, VD), bf), pltpu.VMEM((A, 1, R), jnp.int32),
            pltpu.VMEM((B, R, NOPE), bf), pltpu.VMEM((B, R, ROPE), bf), pltpu.VMEM((B, R, VD), bf),
            pltpu.VMEM((B, 1, R), jnp.int32),
            pltpu.VMEM((1, 3 * NQ), f32), pltpu.VMEM((A, 1, 3 * NQ), f32),
            pltpu.VMEM((A, R, QK), bf), pltpu.VMEM((A, R, QK), bf),
            pltpu.VMEM((B, R, NOPE), bf), pltpu.VMEM((B, R, NOPE), bf),
            pltpu.VMEM((B, R, VD), bf), pltpu.VMEM((B, R, VD), bf),
            pltpu.VMEM((B, R, ROPE), bf), pltpu.VMEM((B * H, R, ROPE), bf),
            pltpu.VMEM((B * H, 1, 128), f32), pltpu.VMEM((A, 1, 128), f32),
            dma((7,)), dma((3, A)), dma((3, A)), dma((4, B)), dma((4, B)), dma((A,)), dma((A,)),
            dma((A,)), dma((A,)), dma((2, B)), dma((2, B)), dma((B, H)), dma((B, H)),
            dma((B, H)), dma((B, H)), dma((A,)), dma((A,)),
        ],
        compiler_params=pltpu.CompilerParams(
            collective_id=0, has_side_effects=True, vmem_limit_bytes=60 * 1024 * 1024
        ),
        name="mla_backward",
    )(query, key_nope, key_rope, value, d_out, positions.reshape(1, R),
      segments.reshape(-1, 128))


def solution(mesh):
    return jax.shard_map(
        shards,
        mesh=mesh,
        in_specs=(
            P("ctx", "head"),
            P("ctx", "head"),
            P("ctx", None),
            P("ctx", "head"),
            P("ctx", "head"),
            P("ctx"),
            P(),
        ),
        out_specs=(P("ctx", "head"), P("ctx", "head"), P("ctx", None), P("ctx", "head")),
        check_vma=False,
    )
```

time: 412 us -> 42.1 us (0.10)
  blocking collectives: 390 us -> 0 us
  Pallas kernels: 0 us -> 35.1 us
  other arithmetic: 6.09 us -> 0 us
  matrix products: 5.77 us -> 0 us
    all_gather x9 -> x0, blocking collectives: 350 us -> none  [the longest x1 45.8 us: shards(): lax.all_gather(key_nope, 'ctx', axis=0, tiled=True)]
    psum x2 -> x0, blocking collectives: 40.2 us -> none  [the longest x1 36.8 us: shards(): total = lax.psum(local_squares, ('ctx', 'head'))]
    pallas_call x0 -> x1, Pallas kernels: none -> 35.1 us  [shards(): pl.pallas_call(functools.partial(kernel, A, B, H, count_all), out_shape=(...]
    dot_general x14 -> x0, matrix products: 5.77 us -> none  [the longest x2 1.35 us: query_advance(): jnp.einsum('hqk,khd->qhd', d_score, key_rows, preferred_element_type=jnp....]
where the time goes in v1:
time: 42.1 us; the launch traced here: 41.7 us
  Pallas kernels  35.1 us (83%)
  local copies, waits for them, and re-layouts  5.89 us (14%)
  between operations  0.66 us (2%)
    pallas_call x1, Pallas kernels, shards(): pl.pallas_call(functools.partial(kernel, A, B, H, count_all), out_shape=(...  35.1 us
    unnamed x12, local copies, waits for them, and re-layouts  3.63 us
    pallas_call x2, local copies, waits for them, and re-layouts, shards(): pl.pallas_call(functools.partial(kernel, A, B, H, count_all), out_shape=(...  2.26 us

profile of v1, /device:TPU:0, one launch (start us, length us, event | category | flops | bytes accessed | tf_op | source)
XLA Modules:
  0.0 41.7 jit_solution(10268760238415969340)
XLA Ops:
  0.6 0.0 copy-start
  0.6 1.4 %copy.12.kr_in = bf16[128,64]{1,0:T(8,128)(2,1)} copy(bf16[128,64]{0,1:T(8,128)(2,1)} %param.9) | data formatting | bytes 32768 | tf_op args[2]
  2.1 0.0 copy-done
  2.1 0.7 %copy.11.q_in = bf16[128,192]{1,0:T(8,128)(2,1)} copy(bf16[128,192]{0,1:T(8,128)(2,1)S(1)} %copy-done) | data formatting | bytes 98304 | tf_op args[0]
  2.8 35.1 %mla_backward.1 = (bf16[128,192]{1,0:T(8,128)(2,1)}, bf16[128,128]{1,0:T(8,128)(2,1)}, bf16[128,64]{1,0:T(8,128)(2,1)}, bf16[128,128]{1,0:T(8,128)(2,1)}) custom-call(bf16[128,192]{1,0:T(8,128)(2,1)} %copy.11.q_in, bf16[128,128]{1,0:T(8,128)(2,1)} %kn_in.1, bf16[128,64]{1,0:T(8,128)(2,1)} %copy.12.kr_in, bf16[128,128]{1,0:T(8,128)(2,1)} %v_in.1, ...), custom_call_target="tpu_custom_call" | custom-call | tf_op jit(solution)/shard_map/mla_backward/pallas_call | solution.py:255
  38.0 0.0 copy-start.1
  38.0 1.6 %copy.13 = bf16[128,192]{0,1:T(8,128)(2,1)} copy(bf16[128,192]{1,0:T(8,128)(2,1)} %get-tuple-element.4) | data formatting | bytes 98304 | tf_op jit(solution)/shard_map/mla_backward/pallas_call | solution.py:255
  39.5 0.0 copy-done.1
  39.5 0.0 copy-start.3
  39.5 0.7 %copy.14 = bf16[128,64]{0,1:T(8,128)(2,1)} copy(bf16[128,64]{1,0:T(8,128)(2,1)S(1)} %copy-done.1) | data formatting | bytes 32768 | tf_op jit(solution)/shard_map/mla_backward/pallas_call | solution.py:255
  40.2 0.1 copy-done.3
  40.3 0.0 copy-start.2
  40.3 0.6 %copy.17 = bf16[128,128]{1,0:T(8,128)(2,1)} copy(bf16[128,128]{1,0:T(8,128)(2,1)S(1)} %copy-done.3) | data formatting | bytes 65536
  40.9 0.2 copy-done.2
  41.1 0.6 %copy.18 = bf16[128,128]{1,0:T(8,128)(2,1)} copy(bf16[128,128]{1,0:T(8,128)(2,1)S(1)} %copy-done.2) | data formatting | bytes 65536
Async XLA Ops:
  0.6 1.5 %copy-start = (bf16[128,192]{0,1:T(8,128)(2,1)S(1)}, bf16[128,192]{0,1:T(8,128)(2,1)}, u32[]{:S(2)}) copy-start(bf16[128,192]{0,1:T(8,128)(2,1)} %param.7) | copy-start | bytes 147460
  38.0 1.6 %copy-start.1 = (bf16[128,64]{1,0:T(8,128)(2,1)S(1)}, bf16[128,64]{1,0:T(8,128)(2,1)}, u32[]{:S(2)}) copy-start(bf16[128,64]{1,0:T(8,128)(2,1)} %get-tuple-element.6) | copy-start | bytes 49156
  39.5 0.8 %copy-start.3 = (bf16[128,128]{1,0:T(8,128)(2,1)S(1)}, bf16[128,128]{1,0:T(8,128)(2,1)}, u32[]{:S(2)}) copy-start(bf16[128,128]{1,0:T(8,128)(2,1)} %get-tuple-element.13) | copy-start | bytes 98308
  40.3 0.8 %copy-start.2 = (bf16[128,128]{1,0:T(8,128)(2,1)S(1)}, bf16[128,128]{1,0:T(8,128)(2,1)}, u32[]{:S(2)}) copy-start(bf16[128,128]{1,0:T(8,128)(2,1)} %get-tuple-element.15) | copy-start | bytes 98308

commit v2 on v1

v2 whole, which is shorter than its diff:
```python
import functools
import math

import jax
import jax.numpy as jnp
from jax import lax
from jax.experimental import pallas as pl
from jax.experimental.pallas import tpu as pltpu
from jax.sharding import PartitionSpec as P

NOPE = 128
ROPE = 64
VD = 128
QK = 192
DOCS = 4
CLIP = 0.25
MESH = pl.DeviceIdType.MESH
HIDDEN = -3.0e38
LOWEST = -1.0e30
STAGE = 9


def grid_of(count):
    width = 1 << (int(math.log2(count)) // 2)
    return count // width, width


def flipped(index, mask, size):
    out, bit = 0, 1
    while bit < size:
        digit = lax.rem(index // bit, 2)
        out = out + bit * ((1 - digit) if mask & bit else digit)
        bit *= 2
    return out


def kernel(
    A, B, H,
    qt_in, kn_in, krt_in, v_in, do_in, pos_in, seg_in,
    out_hbm, part_hbm,
    out, segb,
    qb, dob, pqb, knb, krb, vb, pkb,
    stat, statb,
    dqs, dqr, dks, dkr, dvs, dvr, drs, drr,
    norms,
    own_sem, qsend, qrecv, ksend, krecv, ssend, srecv,
    dqsend, dqrecv, dksend, dkrecv, drsend, drrecv, nsend, nrecv, out_sem,
):
    R = kn_in.shape[0]
    NQ, NK = A * R, B * R
    bf, f32 = jnp.bfloat16, jnp.float32
    scale = 1.0 / math.sqrt(QK)
    ctx = lax.axis_index("ctx")
    head = lax.axis_index("head")
    a, b = ctx // B, ctx % B

    def a_peer(j):
        return {"ctx": lax.rem(a + j + A, A) * B + b, "head": head}

    def b_peer(j, g=0):
        return {"ctx": a * B + flipped(b, j, B), "head": lax.rem(head + g, H)}

    def remote(src, dst, send, recv, peer):
        return pltpu.make_async_remote_copy(
            src_ref=src, dst_ref=dst, send_sem=send, recv_sem=recv,
            device_id=peer, device_id_type=MESH,
        )

    others = [(j, g) for g in range(H) for j in range(B) if (j, g) != (0, 0)]
    barrier = pltpu.get_barrier_semaphore()
    peers = [a_peer(j) for j in range(1, A)] + [b_peer(j, g) for j, g in others]
    for peer in peers:
        pl.semaphore_signal(barrier, inc=1, device_id=peer, device_id_type=MESH)

    own = []
    for i, (src, dst) in enumerate((
        (qt_in, qb.at[0]), (do_in, dob.at[0]), (pos_in, pqb.at[0]),
        (kn_in, knb.at[0]), (krt_in, krb.at[0]), (v_in, vb.at[0]), (pos_in, pkb.at[0]),
        (seg_in, segb),
    )):
        copy = pltpu.make_async_copy(src, dst, own_sem.at[i])
        copy.start()
        own.append(copy)
    for copy in own:
        copy.wait()
    pl.semaphore_wait(barrier, len(peers))
    if STAGE == 0:
        return

    sends = []

    def stop():
        for copy in sends:
            copy.wait_send()

    q_copies, k_copies = [], []
    for j in range(1, max(A, B)):
        if j < A:
            for i, buf in enumerate((qb, pqb, dob)):
                q_copies.append(
                    remote(buf.at[0], buf.at[j], qsend.at[i, j], qrecv.at[i, j], a_peer(j)))
                q_copies[-1].start()
        if j < B:
            for i, buf in enumerate((knb, krb, pkb, vb)):
                k_copies.append(
                    remote(buf.at[0], buf.at[j], ksend.at[i, j], krecv.at[i, j], b_peer(j)))
                k_copies[-1].start()
    sends += q_copies + k_copies

    seg = segb[...]
    firsts = [jnp.sum((seg < doc).astype(jnp.int32)) for doc in range(1, DOCS)]
    for copy in q_copies + k_copies:
        copy.wait_recv()
    if STAGE == 1:
        return stop()

    qt = jnp.concatenate([qb[j] for j in range(A)], axis=1)
    do = dob[...].reshape(NQ, VD)
    kr = jnp.concatenate([jnp.transpose(krb[j]) for j in range(B)], axis=0)
    k = jnp.concatenate([knb[...].reshape(NK, NOPE), kr], axis=1)
    v = vb[...].reshape(NK, VD)
    pos_q = jnp.concatenate([pqb[j] for j in range(A)], axis=1)
    start_q = jnp.zeros_like(pos_q)
    for first in firsts:
        start_q = jnp.where(pos_q >= first, first, start_q)
    pos_k = jnp.concatenate(
        [jnp.transpose(jnp.broadcast_to(pkb[j], (R, R))) for j in range(B)], axis=0)
    pos_k = jnp.concatenate([pos_k] * A, axis=1)

    nt = (((1,), (1,)), ((), ()))
    s = jnp.dot(k, qt, preferred_element_type=f32) * scale
    dp = lax.dot_general(v, do, nt, preferred_element_type=f32)
    vis = (pos_k <= pos_q) & (pos_k >= start_q)
    s = jnp.where(vis, s, HIDDEN)
    m = jnp.maximum(jnp.max(s, axis=0, keepdims=True), LOWEST)
    e = jnp.exp(s - m)
    l = jnp.sum(e, axis=0, keepdims=True)
    wd = jnp.sum(e * dp, axis=0, keepdims=True)

    stat[...] = jnp.concatenate([m, l, wd], axis=1)
    if STAGE == 2:
        return stop()
    s_copies = []
    for j in range(1, A):
        s_copies.append(remote(stat, statb.at[j], ssend.at[j], srecv.at[j], a_peer(j)))
        s_copies[-1].start()
    sends += s_copies
    ms, ls, wds = [m], [l], [wd]
    for copy in s_copies:
        copy.wait_recv()
    if STAGE == 3:
        return stop()
    for j in range(1, A):
        got = statb[j]
        parts = []
        for i in range(3):
            one = got[:, i * NQ:(i + 1) * NQ]
            cut = ((A - j) % A) * R
            parts.append(jnp.concatenate([one[:, cut:], one[:, :cut]], axis=1))
        ms.append(parts[0])
        ls.append(parts[1])
        wds.append(parts[2])
    top = functools.reduce(jnp.maximum, ms)
    shrink = [jnp.exp(x - top) for x in ms]
    total_l = sum(x * y for x, y in zip(ls, shrink))
    total_wd = sum(x * y for x, y in zip(wds, shrink))
    inverse = 1.0 / total_l
    f = shrink[0] * inverse
    delta = total_wd * inverse

    w = e * f
    ds = (w * (dp - delta)).astype(bf)
    kt = jnp.concatenate(
        [jnp.concatenate([jnp.transpose(knb[j]) for j in range(B)], axis=1),
         jnp.concatenate([krb[j] for j in range(B)], axis=1)], axis=0)
    dqt = jnp.dot(kt, ds, preferred_element_type=f32) * scale
    q_grads = []
    for j in range(1, A):
        dqs[j] = dqt[:, j * R:(j + 1) * R].astype(bf)
        q_grads.append(remote(dqs.at[j], dqr.at[j], dqsend.at[j], dqrecv.at[j], a_peer(-j)))
        q_grads[-1].start()
    g_copies = []
    rope_slot = b * H + head
    dv = jnp.dot(w.astype(bf), do, preferred_element_type=f32)
    dvs[...] = dv.astype(bf).reshape(B, R, VD)
    for j in range(1, B):
        g_copies.append(remote(dvs.at[j], dvr.at[j], dksend.at[1, j], dkrecv.at[1, j], b_peer(j)))
        g_copies[-1].start()
    dk = lax.dot_general(ds, qt, nt, preferred_element_type=f32) * scale
    drt = []
    for j in range(B):
        drt.append(jnp.transpose(dk[j * R:(j + 1) * R, NOPE:]).astype(bf))
        drs[j] = drt[j]
    dks[...] = dk[:, :NOPE].astype(bf).reshape(B, R, NOPE)
    for j, g in others:
        g_copies.append(remote(
            drs.at[j], drr.at[rope_slot], drsend.at[j, g], drrecv.at[j, g], b_peer(j, H - g)))
    for j in range(1, B):
        g_copies.append(remote(dks.at[j], dkr.at[j], dksend.at[0, j], dkrecv.at[0, j], b_peer(j)))
    for copy in g_copies[B - 1:]:
        copy.start()
    sends += g_copies + q_grads
    drr[rope_slot] = drt[0]

    for copy in g_copies[: B - 1] + g_copies[len(g_copies) - B + 1:]:
        copy.wait_recv()
    gk = dk[:R, :NOPE]
    gv = dv[:R]
    for j in range(1, B):
        gk = gk + dkr[j].astype(f32)
        gv = gv + dvr[j].astype(f32)
    for j, g in others:
        slot = flipped(b, j, B) * H + lax.rem(head + g, H)
        remote(drs.at[j], drr.at[slot], drsend.at[j, g], drrecv.at[j, g], b_peer(j, g)).wait_recv()
    gr = drr[0].astype(f32)
    for i in range(1, B * H):
        gr = gr + drr[i].astype(f32)
    for copy in q_grads:
        copy.wait_recv()
    gq = dqt[:, :R]
    for j in range(1, A):
        gq = gq + dqr[j].astype(f32)

    def squares(x):
        return jnp.sum(x * x, axis=0, keepdims=True)

    first_head = (head == 0).astype(f32)
    mine = squares(gk) + squares(gv) + squares(gq) + squares(gr) * first_head
    place = ctx * H + head
    norms[place] = mine
    everyone = [(i, j, g) for g in range(H) for i in range(A) for j in range(B) if (i, j, g) != (0, 0, 0)]

    def norm_copy(i, j, g, slot, way):
        peer = {"ctx": lax.rem(a + way * i + A, A) * B + flipped(b, j, B),
                "head": lax.rem(head + way * g + H, H)}
        slot = peer["ctx"] * H + peer["head"] if slot is None else slot
        return remote(norms.at[slot], norms.at[slot], nsend.at[i, j, g], nrecv.at[i, j, g], peer)

    if STAGE != 5:
        for i, j, g in everyone:
            sends.append(norm_copy(i, j, g, place, 1))
            sends[-1].start()
    top_q, top_k, top_r = QK, QK + R, QK + R + ROPE
    out[:top_q, :] = gq
    out[top_q:top_k, :] = gk
    out[top_k:top_r, :] = gr
    out[top_r:, :] = gv
    put = pltpu.make_async_copy(out, out_hbm, out_sem.at[0])
    put.start()
    if STAGE != 5:
        for i, j, g in everyone:
            norm_copy(i, j, g, None, -1).wait_recv()
    part = pltpu.make_async_copy(norms, part_hbm, out_sem.at[1])
    part.start()
    put.wait()
    part.wait()
    stop()


def finish(count_all, grads, part, dq_out, dkn_out, dkr_out, dv_out):
    total = jnp.sum(jnp.sum(part[...], axis=0), axis=1, keepdims=True)
    factor = jnp.minimum(1.0, CLIP * math.sqrt(count_all) / jnp.sqrt(total))
    row = 0
    for dst in (dq_out, dkn_out, dkr_out, dv_out):
        rows = dst.shape[0]
        dst[...] = (grads[row:row + rows, :] * factor).astype(dst.dtype)
        row += rows


def shards(query, key_nope, key_rope, value, d_out, positions, segments):
    R = query.shape[0]
    n, H = lax.axis_size("ctx"), lax.axis_size("head")
    A, B = grid_of(n)
    NQ = A * R
    count_all = float(R * n * (H * (QK + NOPE + VD) + ROPE))
    bf, f32 = jnp.bfloat16, jnp.float32
    any_spec = pl.BlockSpec(memory_space=pl.ANY)
    vmem = pl.BlockSpec(memory_space=pltpu.VMEM)
    dma = pltpu.SemaphoreType.DMA
    rows = QK + R + ROPE + R
    grads, part = pl.pallas_call(
        functools.partial(kernel, A, B, H),
        out_shape=(
            jax.ShapeDtypeStruct((rows, R), f32),
            jax.ShapeDtypeStruct((n * H, 1, 128), f32),
        ),
        in_specs=[any_spec] * 7,
        out_specs=(any_spec, any_spec),
        scratch_shapes=[
            pltpu.VMEM((rows, R), f32), pltpu.VMEM((n * R // 128, 128), jnp.int32),
            pltpu.VMEM((A, QK, R), bf), pltpu.VMEM((A, R, VD), bf), pltpu.VMEM((A, 1, R), jnp.int32),
            pltpu.VMEM((B, R, NOPE), bf), pltpu.VMEM((B, ROPE, R), bf), pltpu.VMEM((B, R, VD), bf),
            pltpu.VMEM((B, 1, R), jnp.int32),
            pltpu.VMEM((1, 3 * NQ), f32), pltpu.VMEM((A, 1, 3 * NQ), f32),
            pltpu.VMEM((A, QK, R), bf), pltpu.VMEM((A, QK, R), bf),
            pltpu.VMEM((B, R, NOPE), bf), pltpu.VMEM((B, R, NOPE), bf),
            pltpu.VMEM((B, R, VD), bf), pltpu.VMEM((B, R, VD), bf),
            pltpu.VMEM((B, ROPE, R), bf), pltpu.VMEM((B * H, ROPE, R), bf),
            pltpu.VMEM((n * H, 1, 128), f32),
            dma((8,)), dma((3, A)), dma((3, A)), dma((4, B)), dma((4, B)), dma((A,)), dma((A,)),
            dma((A,)), dma((A,)), dma((2, B)), dma((2, B)), dma((B, H)), dma((B, H)),
            dma((A, B, H)), dma((A, B, H)), dma((2,)),
        ],
        compiler_params=pltpu.CompilerParams(
            collective_id=0, has_side_effects=True, vmem_limit_bytes=60 * 1024 * 1024
        ),
        name="mla_backward",
    )(query.T, key_nope, key_rope.T, value, d_out, positions.reshape(1, R),
      segments.reshape(-1, 128))
    dqt, dkn, dkrt, dv = pl.pallas_call(
        functools.partial(finish, count_all),
        out_shape=(
            jax.ShapeDtypeStruct((QK, R), bf),
            jax.ShapeDtypeStruct((R, NOPE), bf),
            jax.ShapeDtypeStruct((ROPE, R), bf),
            jax.ShapeDtypeStruct((R, VD), bf),
        ),
        in_specs=[vmem, vmem],
        out_specs=(vmem,) * 4,
        name="clip",
    )(grads, part)
    return dqt.T, dkn, dkrt.T, dv


def solution(mesh):
    return jax.shard_map(
        shards,
        mesh=mesh,
        in_specs=(
            P("ctx", "head"),
            P("ctx", "head"),
            P("ctx", None),
            P("ctx", "head"),
            P("ctx", "head"),
            P("ctx"),
            P(),
        ),
        out_specs=(P("ctx", "head"), P("ctx", "head"), P("ctx", None), P("ctx", "head")),
        check_vma=False,
    )
```

time: 42.1 us -> 33.4 us (0.79)
  local copies, waits for them, and re-layouts: 5.89 us -> 0 us
  Pallas kernels: 35.1 us -> 32.5 us
    unnamed x12 -> x0, local copies, waits for them, and re-layouts: 3.63 us -> none
    pallas_call x1 -> x2, Pallas kernels: 35.1 us -> 32.5 us  [the longest x1 30.8 us: shards(): pl.pallas_call(functools.partial(kernel, A, B, H), out_shape=(jax.ShapeDt...]
    pallas_call x2 -> x0, local copies, waits for them, and re-layouts: 2.26 us -> none  [shards(): pl.pallas_call(functools.partial(kernel, A, B, H, count_all), out_shape=(...]
where the time goes in v2:
time: 33.4 us; the launch traced here: 33.2 us
  Pallas kernels  32.5 us (97%)
  between operations  0.64 us (2%)
    pallas_call x1, Pallas kernels, shards(): pl.pallas_call(functools.partial(kernel, A, B, H), out_shape=(jax.ShapeDt...  30.8 us
    pallas_call x1, Pallas kernels, shards(): pl.pallas_call(functools.partial(finish, count_all), out_shape=(jax.Shape...  1.73 us

profile of v2, /device:TPU:0, one launch (start us, length us, event | category | flops | bytes accessed | tf_op | source)
XLA Modules:
  0.0 33.2 jit_solution(18390693834134456700)
XLA Ops:
  0.6 30.8 %mla_backward.1 = (f32[512,128]{1,0:T(8,128)}, f32[32,1,128]{2,1,0:T(1,128)}) custom-call(bf16[192,128]{1,0:T(8,128)(2,1)} %bitcast.6, bf16[128,128]{1,0:T(8,128)(2,1)} %kn_in.1, bf16[64,128]{1,0:T(8,128)(2,1)} %bitcast.7, bf16[128,128]{1,0:T(8,128)(2,1)} %v_in.1, bf16[128,128]{1,0:T(8,128)(2,1)} %do_in.1, s32[1,128]{1,0:T(1,128)} %bitcast.9, s32[16,128]{1,0:T(8,128)} %bitcast.8), custom_call_target="tpu_custom_call" | custom-call | tf_op jit(solution)/shard_map/mla_backward/pallas_call | solution.py:281
  31.5 1.7 %clip.1 = (bf16[192,128]{1,0:T(8,128)(2,1)}, bf16[128,128]{1,0:T(8,128)(2,1)}, bf16[64,128]{1,0:T(8,128)(2,1)}, bf16[128,128]{1,0:T(8,128)(2,1)}) custom-call(f32[512,128]{1,0:T(8,128)} %get-tuple-element.10.grads, f32[32,1,128]{2,1,0:T(1,128)} %get-tuple-element.11.part), custom_call_target="tpu_custom_call" | custom-call | tf_op jit(solution)/shard_map/clip/pallas_call | solution.py:310
